TPU v7x, 128 devices: a whole 4x4x4 slice. The times are simulated.
128 devices in a mesh: seq: 64 (over x, y, z), head: 2 (over core).
Axes of the slice: x: 4, y: 4, z: 4, core: 2. Of those that a mesh axis runs over, the one named last changes fastest.
Arguments:
- tokens: bfloat16 [65536, 2048], P('seq'), may hold values from -6 to 6
- w_query: bfloat16 [2048, 256], P(None, 'head'), may hold values from -0.25 to 0.25
- w_key: bfloat16 [2048, 256], P(None, 'head'), may hold values from -0.25 to 0.25
- w_value: bfloat16 [2048, 2048], P(None, 'head'), may hold values from -0.125 to 0.125
- w_out: bfloat16 [2048, 2048], replicated, may hold values from -1.796875 to 1.796875
Outputs:
- mixed: bfloat16 [65536, 2048], P('seq', 'head')
All inputs are finite; a program needn't handle non-finite values.
Results may differ from a plain program's by a relative error of at most 0.011.
Values may be sent and summed in bfloat16 or wider, within the bound.
A program may use at most 128 MiB of HBM per device.

v0:
```python
import jax
import jax.numpy as jnp
from jax import lax
from jax.experimental import pallas as pl
from jax.experimental.pallas import tpu as pltpu
from jax.sharding import PartitionSpec as P

TOK = 1024
D = 2048
HERE = 8
CHUNK = 256
NCH = TOK // CHUNK
FEAT = 160
HALF = FEAT // 2
PLANE = 16
XN = 4
MESH = pl.DeviceIdType.MESH
C2 = 1.0 / (32.0**0.5)
BF = jnp.bfloat16
F32 = jnp.float32


def dot(a, b):
    return jnp.dot(a, b, preferred_element_type=F32)


def iota(shape, dim):
    return lax.broadcasted_iota(jnp.int32, shape, dim)


def kernel(
    tok_hbm, wq_hbm, wk_hbm, wv_hbm, wo_hbm, out_hbm,
    tok, wqk, wv, wo, q_s, kt, ktb, v_s, phiq, pk, ea, eb, lext, numer,
    sbuf, rbuf, xs, xbuf, obuf, pbuf, att, outv,
    tok_sem, wqk_sem, wv_sem, wo_sem, out_sem,
    s_send, s_recv, x_send, x_recv, p_send, p_recv, a_send, a_recv,
):
    seq = lax.axis_index("seq")
    core = lax.axis_index("head")
    xp = seq // PLANE
    me = lax.rem(seq, PLANE)

    def wqk_copy(j):
        src = (wq_hbm, wk_hbm)[j]
        return pltpu.make_async_copy(src, wqk.at[:, pl.ds(j * 128, 128)], wqk_sem.at[j])

    def tok_copy(b):
        rows = pl.ds(b * CHUNK, CHUNK)
        return pltpu.make_async_copy(tok_hbm.at[rows, :], tok.at[rows, :], tok_sem.at[b])

    def wv_copy(j):
        cols = pl.ds(pl.multiple_of(j * 256, 256), 256)
        return pltpu.make_async_copy(wv_hbm.at[:, cols], wv.at[j], wv_sem.at[j])

    def wo_copy(j):
        cols = pl.ds(pl.multiple_of(core * 1024 + j * 256, 256), 256)
        return pltpu.make_async_copy(wo_hbm.at[:, cols], wo.at[j], wo_sem.at[j])

    for j in range(2):
        wqk_copy(j).start()
    for b in range(NCH):
        tok_copy(b).start()
    for j in range(4):
        wv_copy(j).start()
    for j in range(4):
        wo_copy(j).start()

    barrier = pltpu.get_barrier_semaphore()

    def greet(i, c):
        @pl.when(i != me)
        def _():
            pl.semaphore_signal(
                barrier, inc=1, device_id={"seq": xp * PLANE + i}, device_id_type=MESH
            )

        return c

    lax.fori_loop(0, PLANE, greet, 0)
    for dx in range(1, XN):
        pl.semaphore_signal(
            barrier,
            inc=1,
            device_id={"seq": lax.rem(xp + dx, XN) * PLANE + me},
            device_id_type=MESH,
        )
    pl.semaphore_signal(barrier, inc=1, device_id={"head": 1 - core}, device_id_type=MESH)

    row = iota((256, 256), 0)
    col = iota((256, 256), 1)
    lane_i = col & 15
    lane_d = (col >> 4) - 1
    ea[...] = jnp.where((row == 128 + lane_i) & (col < 152), 1.0, 0.0).astype(BF)
    eb[...] = jnp.where(
        (row == 128 + ((lane_i + lane_d) & 15)) & (col >= 16) & (col < 152), 1.0, 0.0
    ).astype(BF)

    for j in range(2):
        wqk_copy(j).wait()
    for b in range(NCH):
        tok_copy(b).wait()
        rows = slice(b * CHUNK, (b + 1) * CHUNK)
        qk = dot(tok[rows, :], wqk[...])
        q_s[rows, :] = qk[:, :128].astype(BF)
        k_t = qk[:, 128:].astype(BF).astype(F32).T
        kt[:, rows] = k_t
        ktb[:, rows] = k_t.astype(BF)

    pl.semaphore_wait(barrier, PLANE - 1 + XN - 1 + 1)

    eye = iota((128, 128), 0) == iota((128, 128), 1)
    ones = jnp.ones((CHUNK, 128), BF)
    row16 = iota((16, 128), 0)
    row16w = iota((16, TOK), 0)

    def state_copy(o):
        return pltpu.make_async_remote_copy(
            src_ref=sbuf.at[o], dst_ref=rbuf.at[me], send_sem=s_send.at[o],
            recv_sem=s_recv.at[me], device_id={"seq": xp * PLANE + o}, device_id_type=MESH,
        )

    def state_arrival(q):
        return pltpu.make_async_remote_copy(
            src_ref=sbuf.at[q], dst_ref=rbuf.at[q], send_sem=s_send.at[q],
            recv_sem=s_recv.at[q], device_id={"seq": xp * PLANE + q}, device_id_type=MESH,
        )

    def total_copy(dx):
        return pltpu.make_async_remote_copy(
            src_ref=xs, dst_ref=xbuf.at[xp], send_sem=x_send.at[dx - 1], recv_sem=x_recv.at[xp],
            device_id={"seq": lax.rem(xp + dx, XN) * PLANE + me}, device_id_type=MESH,
        )

    def total_arrival(dx):
        other = lax.rem(xp + dx, XN)
        return pltpu.make_async_remote_copy(
            src_ref=xs, dst_ref=xbuf.at[other], send_sem=x_send.at[dx - 1],
            recv_sem=x_recv.at[other], device_id={"seq": other * PLANE + me}, device_id_type=MESH,
        )

    def prefix_copy(q):
        return pltpu.make_async_remote_copy(
            src_ref=obuf.at[q], dst_ref=pbuf.at[me], send_sem=p_send.at[q],
            recv_sem=p_recv.at[me], device_id={"seq": xp * PLANE + q}, device_id_type=MESH,
        )

    def prefix_arrival(o):
        return pltpu.make_async_remote_copy(
            src_ref=obuf.at[o], dst_ref=pbuf.at[o], send_sem=p_send.at[o],
            recv_sem=p_recv.at[o], device_id={"seq": xp * PLANE + o}, device_id_type=MESH,
        )

    def att_copy(h, side):
        cols = pl.ds(pl.multiple_of((side * HERE + h) * 128, 128), 128)
        return pltpu.make_async_remote_copy(
            src_ref=att.at[:, cols], dst_ref=att.at[:, cols], send_sem=a_send.at[h],
            recv_sem=a_recv.at[h], device_id={"head": 1 - core}, device_id_type=MESH,
        )

    def pair(hp, c):
        wv_copy(hp).wait()
        v_s[hp] = dot(tok[...], wv[hp]).astype(BF)
        for j in range(2):
            h = 2 * hp + j
            u = kt[pl.ds(pl.multiple_of(h * 16, 16), 16), :]
            pk[j, 0:16, :] = (u * 0.5).astype(BF)
            for d in range(8):
                other = u if d == 0 else pltpu.roll(u, 16 - d, 0)
                pk[j, 16 + 16 * d : 32 + 16 * d, :] = (u * other * C2).astype(BF)
            last = u * pltpu.roll(u, 8, 0) * C2
            last = jnp.where(row16w < 8, last, jnp.where(row16w == 8, 1.0, 0.0))
            pk[j, 144:160, :] = last.astype(BF)
        for j in range(2):
            h = 2 * hp + j
            run = None
            for b in range(NCH):
                rows = slice(b * CHUNK, (b + 1) * CHUNK)
                vals = jnp.concatenate([v_s[hp, rows, j * 128 : (j + 1) * 128], ones], axis=1)
                part = dot(pk[j, :, rows], vals)
                run = part if run is None else run + part
                if b < NCH - 1:
                    lext[h, b] = run.astype(BF)
            zc = run[:, 128:]
            z0 = jnp.sum(jnp.where(eye, zc[:128], 0.0), axis=0, keepdims=True)
            z1 = jnp.sum(jnp.where(eye[:32], zc[128:], 0.0), axis=0, keepdims=True)
            tail = jnp.where(row16 == 14, z0, jnp.where(row16 == 15, z1, run[144:160, :128]))
            sbuf[2 * h] = run[:HALF, :128].astype(BF)
            sbuf[2 * h + 1, 0:64, :] = run[HALF:144, :128].astype(BF)
            sbuf[2 * h + 1, 64:80, :] = tail.astype(BF)
        for j in range(4):
            o = 4 * hp + j

            @pl.when(o != me)
            def _():
                state_copy(o).start()

            @pl.when(o == me)
            def _():
                rbuf[me] = sbuf[o]

        return c

    lax.fori_loop(0, 4, pair, 0)

    lane = iota((1, 256), 1)
    c1 = jnp.where(lane < 16, 1.0, 0.0)
    c0 = jnp.where(lane == 152, 2.0, 0.0)
    scale = jnp.where(lane < 16, 1.0, jnp.where(lane < 32, 2.0 * C2, 4.0 * C2))
    lane128 = iota((1, 128), 1)
    causal = iota((CHUNK, CHUNK), 1) <= iota((CHUNK, CHUNK), 0)

    def inside(h, c):
        low = pl.multiple_of(128 - 16 * h, 16)
        ea_h = ea[pl.ds(low, 128), :]
        eb_h = eb[pl.ds(low, 128), :]
        own = jnp.where((lane128 >> 4) == h, 0.25, 0.0).astype(BF)
        hp = h // 2
        vcols = pl.ds(pl.multiple_of(lax.rem(h, 2) * 128, 128), 128)
        for b in range(NCH):
            rows = slice(b * CHUNK, (b + 1) * CHUNK)
            qb = q_s[rows, :]
            first = dot(qb, ea_h)
            second = dot(qb, eb_h)
            feat = (first * (second + c1) * scale + c0).astype(BF)
            phiq[h, rows, :] = feat
            t = dot(qb * own, ktb[:, rows]) + 1.0
            t = jnp.where(causal, t * t + 1.0, 0.0).astype(BF)
            vals = jnp.concatenate([v_s[hp, rows, vcols], ones], axis=1)
            r = dot(t, vals)
            if b > 0:
                r = r + dot(feat[:, :FEAT], lext[h, b - 1])
            numer[h, rows, :] = r
        return c

    def owner_reduce():
        def arrive(q, c):
            @pl.when(q != me)
            def _():
                state_arrival(q).wait_recv()

            return c

        lax.fori_loop(0, PLANE, arrive, 0)
        tot = lax.fori_loop(
            0, PLANE, lambda q, a: a + rbuf[q].astype(F32), jnp.zeros((HALF, 128), F32)
        )
        xs[...] = tot.astype(BF)
        for dx in range(1, XN):
            total_copy(dx).start()

    def owner_prefix():
        for dx in range(1, XN):
            total_arrival(dx).wait_recv()
        base = lax.fori_loop(
            0, xp, lambda k, a: a + xbuf[k].astype(F32), jnp.zeros((HALF, 128), F32)
        )

        def step(q, a):
            obuf[q] = a.astype(BF)
            return a + rbuf[q].astype(F32)

        lax.fori_loop(0, PLANE, step, base)

        def give(q, c):
            @pl.when(q != me)
            def _():
                prefix_copy(q).start()

            @pl.when(q == me)
            def _():
                pbuf[me] = obuf[q]

            return c

        lax.fori_loop(0, PLANE, give, 0)

    lax.fori_loop(0, 4, inside, 0)
    owner_reduce()
    lax.fori_loop(4, 6, inside, 0)
    owner_prefix()
    lax.fori_loop(6, 8, inside, 0)

    ones128 = jnp.ones((128, 128), BF)

    def finish(h, c):
        for j in range(2):
            o = 2 * h + j

            @pl.when(o != me)
            def _():
                prefix_arrival(o).wait_recv()

        top = pbuf[2 * h]
        bottom = pbuf[2 * h + 1]
        zz = bottom[64:80].astype(F32)
        m0 = jnp.where(eye, zz[14:15], 0.0).astype(BF)
        m1 = jnp.where(eye[:32], zz[15:16], 0.0).astype(BF)
        zb = dot(jnp.concatenate([m0, m1], axis=0), ones128).astype(BF)
        pre = jnp.concatenate([jnp.concatenate([top, bottom], axis=0), zb], axis=1)
        cols = pl.ds(pl.multiple_of((core * HERE + h) * 128, 128), 128)
        for b in range(NCH):
            rows = slice(b * CHUNK, (b + 1) * CHUNK)
            r = dot(phiq[h, rows, :FEAT], pre) + numer[h, rows, :]
            att[rows, cols] = (r[:, :128] / r[:, 128:]).astype(BF)
        att_copy(h, core).start()
        return c

    lax.fori_loop(0, HERE, finish, 0)

    for h in range(HERE):
        att_copy(h, 1 - core).wait_recv()

    def out_copy(j):
        cols = pl.ds(pl.multiple_of(j * 256, 256), 256)
        return pltpu.make_async_copy(outv.at[j], out_hbm.at[:, cols], out_sem.at[j])

    def project(j, c):
        wo_copy(j).wait()
        outv[j] = dot(att[...], wo[j]).astype(BF)
        out_copy(j).start()
        return c

    lax.fori_loop(0, 4, project, 0)

    def drain(q, c):
        @pl.when(q != me)
        def _():
            state_copy(q).wait_send()
            prefix_copy(q).wait_send()

        return c

    lax.fori_loop(0, PLANE, drain, 0)
    for dx in range(1, XN):
        total_copy(dx).wait_send()
    for h in range(HERE):
        att_copy(h, core).wait_send()
    for j in range(4):
        out_copy(j).wait()


def per_device(tokens, w_query, w_key, w_value, w_out):
    vmem = pltpu.VMEM
    dma = pltpu.SemaphoreType.DMA
    hbm = pl.BlockSpec(memory_space=pl.ANY)
    return pl.pallas_call(
        kernel,
        out_shape=jax.ShapeDtypeStruct((TOK, 1024), BF),
        in_specs=[hbm] * 5,
        out_specs=hbm,
        scratch_shapes=[
            vmem((TOK, D), BF),
            vmem((D, 256), BF),
            vmem((4, D, 256), BF),
            vmem((4, D, 256), BF),
            vmem((TOK, 128), BF),
            vmem((128, TOK), F32),
            vmem((128, TOK), BF),
            vmem((4, TOK, 256), BF),
            vmem((HERE, TOK, 256), BF),
            vmem((2, FEAT, TOK), BF),
            vmem((256, 256), BF),
            vmem((256, 256), BF),
            vmem((HERE, NCH - 1, FEAT, 256), BF),
            vmem((HERE, TOK, 256), F32),
            vmem((PLANE, HALF, 128), BF),
            vmem((PLANE, HALF, 128), BF),
            vmem((HALF, 128), BF),
            vmem((XN, HALF, 128), BF),
            vmem((PLANE, HALF, 128), BF),
            vmem((PLANE, HALF, 128), BF),
            vmem((TOK, D), BF),
            vmem((4, TOK, 256), BF),
            dma((NCH,)), dma((2,)), dma((4,)), dma((4,)), dma((4,)),
            dma((PLANE,)), dma((PLANE,)), dma((XN,)), dma((XN,)),
            dma((PLANE,)), dma((PLANE,)), dma((HERE,)), dma((HERE,)),
        ],
        compiler_params=pltpu.CompilerParams(
            collective_id=0, has_side_effects=True, vmem_limit_bytes=60 * 1024 * 1024
        ),
    )(tokens, w_query, w_key, w_value, w_out)


def solution(mesh):
    in_specs = (P("seq", None), P(None, "head"), P(None, "head"), P(None, "head"), P())
    return jax.shard_map(
        per_device, mesh=mesh, in_specs=in_specs, out_specs=P("seq", "head"), check_vma=False
    )
```

profile of v0, /device:TPU:1, one launch (start us, length us, event | category | flops | bytes accessed | tf_op | source)
XLA Modules:
  0.0 46.8 jit_solution(7893409620433189465)
XLA Ops:
  0.0 43.7 %shard_map.55 = bf16[1024,1024]{1,0:T(8,128)(2,1)} custom-call(bf16[1024,2048]{1,0:T(8,128)(2,1)} %tok_hbm.1, bf16[2048,128]{1,0:T(8,128)(2,1)} %wq_hbm.1, bf16[2048,128]{1,0:T(8,128)(2,1)} %wk_hbm.1, bf16[2048,1024]{1,0:T(8,128)(2,1)} %wv_hbm.1, bf16[2048,2048]{1,0:T(8,128)(2,1)} %wo_hbm.1), custom_call_target="tpu_custom_call" | custom-call | tf_op jit(solution)/shard_map/pallas_call | solution.py:346
  43.7 3.1 %copy.7 = bf16[1024,1024]{1,0:T(8,128)(2,1)} copy(bf16[1024,1024]{1,0:T(8,128)(2,1)} %shard_map.55) | data formatting | bytes 4194304
where the time goes:
time: 46.9 us; the launch traced here: 46.8 us
  Pallas kernels  43.7 us (93%)
  local copies, waits for them, and re-layouts  3.08 us (7%)
    pallas_call x1, Pallas kernels, per_device(): pl.pallas_call(kernel, out_shape=jax.ShapeDtypeStruct((TOK, 1024), BF), i...  43.7 us
    unnamed x1, local copies, waits for them, and re-layouts  3.08 us

commit v1 on v0

v1 whole, which is shorter than its diff:
```python
import jax
import jax.numpy as jnp
from jax import lax
from jax.experimental import pallas as pl
from jax.experimental.pallas import tpu as pltpu
from jax.sharding import PartitionSpec as P

TOK = 1024
D = 2048
HERE = 8
CHUNK = 256
NCH = TOK // CHUNK
FEAT = 160
PIECE = FEAT // 4
PLANE = 16
XN = 4
SHIFTS = sorted(
    [(dy, dz) for dy in range(4) for dz in range(4) if dy or dz],
    key=lambda s: -(min(s[0], 4 - s[0]) + min(s[1], 4 - s[1])),
)
NS = len(SHIFTS)
QK_PARTS = 1
REDUCE_AT = (1, 5)
PREFIX_AT = (5, 8)
MESH = pl.DeviceIdType.MESH
C2 = 1.0 / (32.0**0.5)
BF = jnp.bfloat16
F32 = jnp.float32


def dot(a, b):
    return jnp.dot(a, b, preferred_element_type=F32)


def iota(shape, dim):
    return lax.broadcasted_iota(jnp.int32, shape, dim)


def kernel(
    tok_hbm, wq_hbm, wk_hbm, wv_hbm, wo_hbm, out,
    tok, wqk, wv, wo, q_s, k_s, kt, ktb, v_s, phiq, pk, ea, eb, lext, numer,
    sbuf, rbuf, xs, xbuf, obuf, pbuf, pre, att, sib, acc,
    tok_sem, wqk_sem, wv_sem, wo_sem,
    s_send, s_recv, x_send, x_recv, p_send, p_recv, a_send, a_recv,
):
    seq = lax.axis_index("seq")
    core = lax.axis_index("head")
    xp = seq // PLANE
    me = lax.rem(seq, PLANE)

    def wqk_copy(j):
        src = (wq_hbm, wk_hbm)[j]
        return pltpu.make_async_copy(src, wqk.at[:, pl.ds(j * 128, 128)], wqk_sem.at[j])

    def tok_copy(b):
        rows = pl.ds(b * CHUNK, CHUNK)
        return pltpu.make_async_copy(tok_hbm.at[rows, :], tok.at[rows, :], tok_sem.at[b])

    def wv_copy(j):
        cols = pl.ds(j * 512, 512)
        return pltpu.make_async_copy(wv_hbm.at[:, cols], wv.at[j], wv_sem.at[j])

    def wo_copy(j):
        side, half = j // 2, j % 2
        base = (core if side == 0 else 1 - core) * 1024 + half * 512
        rows = pl.ds(pl.multiple_of(base, 512), 512)
        cols = pl.ds(pl.multiple_of(core * 1024, 1024), 1024)
        return pltpu.make_async_copy(wo_hbm.at[rows, cols], wo.at[j], wo_sem.at[j])

    for j in range(2):
        wqk_copy(j).start()
    for b in range(NCH):
        tok_copy(b).start()

    barrier = pltpu.get_barrier_semaphore()

    def chip(i, sign=1):
        dy, dz = SHIFTS[i]
        y = lax.rem(me // 4 + 4 + sign * dy, 4)
        z = lax.rem(lax.rem(me, 4) + 4 + sign * dz, 4)
        return y * 4 + z

    for i in range(NS):
        pl.semaphore_signal(
            barrier, inc=1, device_id={"seq": xp * PLANE + chip(i)}, device_id_type=MESH
        )
    for dx in range(1, XN):
        pl.semaphore_signal(
            barrier,
            inc=1,
            device_id={"seq": lax.rem(xp + dx, XN) * PLANE + me},
            device_id_type=MESH,
        )
    pl.semaphore_signal(barrier, inc=1, device_id={"head": 1 - core}, device_id_type=MESH)

    row = iota((256, 256), 0)
    col = iota((256, 256), 1)
    lane_i = col & 15
    lane_d = (col >> 4) - 1
    ea[...] = jnp.where((row == 128 + lane_i) & (col < 152), 1.0, 0.0).astype(BF)
    eb[...] = jnp.where(
        (row == 128 + ((lane_i + lane_d) & 15)) & (col >= 16) & (col < 152), 1.0, 0.0
    ).astype(BF)

    for j in range(2):
        wqk_copy(j).wait()
    for part in range(QK_PARTS):
        each = NCH // QK_PARTS
        for b in range(part * each, part * each + each):
            tok_copy(b).wait()
        if part == 0:
            for j in range(2):
                wv_copy(j).start()
        rows = slice(part * each * CHUNK, (part + 1) * each * CHUNK)
        qk = dot(tok[rows, :], wqk[...])
        q_s[rows, :] = qk[:, :128].astype(BF)
        k_s[rows, :] = qk[:, 128:].astype(BF)
    for j in range(4):
        wo_copy(j).start()


    eye = iota((128, 128), 0) == iota((128, 128), 1)
    ones = jnp.ones((CHUNK, 128), BF)
    row_p = iota((PIECE, 128), 0)
    row16w = iota((16, TOK), 0)

    def state_copy(g, i):
        to = chip(i)
        return pltpu.make_async_remote_copy(
            src_ref=sbuf.at[g * PLANE + to], dst_ref=rbuf.at[g, me], send_sem=s_send.at[g, i],
            recv_sem=s_recv.at[g, i], device_id={"seq": xp * PLANE + to}, device_id_type=MESH,
        )

    def state_arrival(g, i):
        come = chip(i, -1)
        return pltpu.make_async_remote_copy(
            src_ref=sbuf.at[g * PLANE + come], dst_ref=rbuf.at[g, come], send_sem=s_send.at[g, i],
            recv_sem=s_recv.at[g, i], device_id={"seq": xp * PLANE + come}, device_id_type=MESH,
        )

    def total_copy(g, dx):
        return pltpu.make_async_remote_copy(
            src_ref=xs.at[g], dst_ref=xbuf.at[g, xp], send_sem=x_send.at[g, dx - 1],
            recv_sem=x_recv.at[g, dx - 1],
            device_id={"seq": lax.rem(xp + dx, XN) * PLANE + me}, device_id_type=MESH,
        )

    def total_arrival(g, dx):
        other = lax.rem(xp + XN - dx, XN)
        return pltpu.make_async_remote_copy(
            src_ref=xs.at[g], dst_ref=xbuf.at[g, other], send_sem=x_send.at[g, dx - 1],
            recv_sem=x_recv.at[g, dx - 1],
            device_id={"seq": other * PLANE + me}, device_id_type=MESH,
        )

    def prefix_copy(g, i):
        to = chip(i)
        return pltpu.make_async_remote_copy(
            src_ref=obuf.at[g, to], dst_ref=pbuf.at[g * PLANE + me], send_sem=p_send.at[g, i],
            recv_sem=p_recv.at[g, i], device_id={"seq": xp * PLANE + to}, device_id_type=MESH,
        )

    def prefix_arrival(g, i):
        come = chip(i, -1)
        return pltpu.make_async_remote_copy(
            src_ref=obuf.at[g, come], dst_ref=pbuf.at[g * PLANE + come], send_sem=p_send.at[g, i],
            recv_sem=p_recv.at[g, i], device_id={"seq": xp * PLANE + come}, device_id_type=MESH,
        )

    def att_copy(h):
        cols = pl.ds(h * 128, 128)
        return pltpu.make_async_remote_copy(
            src_ref=att.at[:, cols], dst_ref=sib.at[:, cols], send_sem=a_send.at[h],
            recv_sem=a_recv.at[h], device_id={"head": 1 - core}, device_id_type=MESH,
        )

    def values(g):
        wv_copy(g).wait()
        if g == 0:
            for b in range(NCH):
                rows = slice(b * CHUNK, (b + 1) * CHUNK)
                k_t = k_s[rows, :].T
                kt[:, rows] = k_t.astype(F32)
                ktb[:, rows] = k_t
        v_s[g] = dot(tok[...], wv[g]).astype(BF)

    def key_features(g):
        for j in range(4):
            h = 4 * g + j
            u = kt[h * 16 : (h + 1) * 16, :]
            pk[j, 0:16, :] = (u * 0.5).astype(BF)
            for d in range(8):
                other = u if d == 0 else pltpu.roll(u, 16 - d, 0)
                pk[j, 16 + 16 * d : 32 + 16 * d, :] = (u * other * C2).astype(BF)
            last = u * pltpu.roll(u, 8, 0) * C2
            last = jnp.where(row16w < 8, last, jnp.where(row16w == 8, 1.0, 0.0))
            pk[j, 144:160, :] = last.astype(BF)

    def states(g):
        for j in range(4):
            h = 4 * g + j
            run = None
            for b in range(NCH):
                rows = slice(b * CHUNK, (b + 1) * CHUNK)
                vals = jnp.concatenate([v_s[g, rows, j * 128 : (j + 1) * 128], ones], axis=1)
                part = dot(pk[j, :, rows], vals)
                run = part if run is None else run + part
                if b < NCH - 1:
                    lext[h, b] = run.astype(BF)
            zc = run[:, 128:]
            z0 = jnp.sum(jnp.where(eye, zc[:128], 0.0), axis=0, keepdims=True)
            z1 = jnp.sum(jnp.where(eye[:32], zc[128:], 0.0), axis=0, keepdims=True)
            for k in range(4):
                piece = run[k * PIECE : (k + 1) * PIECE, :128]
                if k == 3:
                    piece = jnp.where(row_p == 38, z0, jnp.where(row_p == 39, z1, piece))
                sbuf[h * 4 + k] = piece.astype(BF)

    def send_states(g):
        for i in range(NS):
            state_copy(g, i).start()
        rbuf[g, me] = sbuf[g * PLANE + me]

    lane = iota((1, 256), 1)
    c1 = jnp.where(lane < 16, 1.0, 0.0)
    c0 = jnp.where(lane == 152, 2.0, 0.0)
    scale = jnp.where(lane < 16, 1.0, jnp.where(lane < 32, 2.0 * C2, 4.0 * C2))
    lane128 = iota((1, 128), 1)
    causal = iota((CHUNK, CHUNK), 1) <= iota((CHUNK, CHUNK), 0)

    def inside(h):
        low = 128 - 16 * h
        ea_h = ea[low : low + 128, :]
        eb_h = eb[low : low + 128, :]
        own = jnp.where((lane128 >> 4) == h, 0.25, 0.0).astype(BF)
        vcols = slice((h % 4) * 128, (h % 4) * 128 + 128)
        for b in range(NCH):
            rows = slice(b * CHUNK, (b + 1) * CHUNK)
            qb = q_s[rows, :]
            first = dot(qb, ea_h)
            second = dot(qb, eb_h)
            feat = (first * (second + c1) * scale + c0).astype(BF)
            phiq[h, rows, :] = feat
            t = dot(qb * own, ktb[:, rows]) + 1.0
            t = jnp.where(causal, t * t + 1.0, 0.0).astype(BF)
            vals = jnp.concatenate([v_s[h // 4, rows, vcols], ones], axis=1)
            r = dot(t, vals)
            if b > 0:
                r = r + dot(feat[:, :FEAT], lext[h, b - 1])
            numer[h, rows, :] = r

    def reduce_step(g):
        for i in range(NS):
            state_arrival(g, i).wait_recv()
        tot = rbuf[g, 0].astype(F32)
        for q in range(1, PLANE):
            tot = tot + rbuf[g, q].astype(F32)
        xs[g] = tot.astype(BF)
        for dx in range(1, XN):
            pl.when(xp + dx < XN)(total_copy(g, dx).start)

    def prefix_step(g):
        for dx in range(1, XN):
            pl.when(xp >= dx)(total_arrival(g, dx).wait_recv)
        run = lax.fori_loop(
            0, xp, lambda k, a: a + xbuf[g, k].astype(F32), jnp.zeros((PIECE, 128), F32)
        )
        for q in range(PLANE):
            obuf[g, q] = run.astype(BF)
            run = run + rbuf[g, q].astype(F32)
        for i in range(NS):
            prefix_copy(g, i).start()
        pbuf[g * PLANE + me] = obuf[g, me]

    def slot(i):
        for g in range(2):
            if REDUCE_AT[g] == i:
                reduce_step(g)
            if PREFIX_AT[g] == i:
                prefix_step(g)

    ones128 = jnp.ones((128, 128), BF)

    def finish(g):
        for i in range(NS):
            prefix_arrival(g, i).wait_recv()
        for h in range(4 * g, 4 * g + 4):
            pieces = [pbuf[4 * h + k].astype(F32) for k in range(4)]
            z = pieces[3][38:40]
            m = jnp.concatenate(
                [jnp.where(eye, z[0:1], 0.0), jnp.where(eye[:32], z[1:2], 0.0)], axis=0
            )
            pre[h, :, :128] = jnp.concatenate(pieces, axis=0).astype(BF)
            pre[h, :, 128:] = dot(m.astype(BF), ones128).astype(BF)
        for h in range(4 * g, 4 * g + 4):
            for b in range(NCH):
                rows = slice(b * CHUNK, (b + 1) * CHUNK)
                r = dot(phiq[h, rows, :FEAT], pre[h]) + numer[h, rows, :]
                att[rows, h * 128 : (h + 1) * 128] = (r[:, :128] / r[:, 128:]).astype(BF)
            att_copy(h).start()

    def project(side, half, step):
        j = side * 2 + half
        wo_copy(j).wait()
        if side == 1:
            for h in range(4 * half, 4 * half + 4):
                att_copy(h).wait_recv()
        lhs = (att, sib)[side]
        for n in range(4):
            cols = slice(n * 256, (n + 1) * 256)
            r = dot(lhs[:, half * 512 : (half + 1) * 512], wo[j, :, cols])
            if step > 0:
                r = r + acc[:, cols]
            if step < 3:
                acc[:, cols] = r
            else:
                out[:, cols] = r.astype(BF)

    for g in range(2):
        values(g)
        key_features(g)
        states(g)
        if g == 0:
            pl.semaphore_wait(barrier, NS + XN - 1 + 1)
        send_states(g)
    slot(0)
    for h in range(HERE):
        inside(h)
        slot(h + 1)
    finish(0)
    project(0, 0, 0)
    project(1, 0, 1)
    finish(1)
    project(0, 1, 2)
    project(1, 1, 3)

    for g in range(2):
        for i in range(NS):
            state_copy(g, i).wait_send()
            prefix_copy(g, i).wait_send()
        for dx in range(1, XN):
            pl.when(xp + dx < XN)(total_copy(g, dx).wait_send)
    for h in range(HERE):
        att_copy(h).wait_send()


def per_device(tokens, w_query, w_key, w_value, w_out):
    vmem = pltpu.VMEM
    dma = pltpu.SemaphoreType.DMA
    hbm = pl.BlockSpec(memory_space=pl.ANY)
    return pl.pallas_call(
        kernel,
        out_shape=pltpu.VMEM((TOK, 1024), BF),
        in_specs=[hbm] * 5,
        out_specs=pl.BlockSpec(memory_space=pltpu.VMEM),
        scratch_shapes=[
            vmem((TOK, D), BF),
            vmem((D, 256), BF),
            vmem((2, D, 512), BF),
            vmem((4, 512, 1024), BF),
            vmem((TOK, 128), BF),
            vmem((TOK, 128), BF),
            vmem((128, TOK), F32),
            vmem((128, TOK), BF),
            vmem((2, TOK, 512), BF),
            vmem((HERE, TOK, 256), BF),
            vmem((4, FEAT, TOK), BF),
            vmem((256, 256), BF),
            vmem((256, 256), BF),
            vmem((HERE, NCH - 1, FEAT, 256), BF),
            vmem((HERE, TOK, 256), F32),
            vmem((2 * PLANE, PIECE, 128), BF),
            vmem((2, PLANE, PIECE, 128), BF),
            vmem((2, PIECE, 128), BF),
            vmem((2, XN, PIECE, 128), BF),
            vmem((2, PLANE, PIECE, 128), BF),
            vmem((2 * PLANE, PIECE, 128), BF),
            vmem((HERE, FEAT, 256), BF),
            vmem((TOK, 1024), BF),
            vmem((TOK, 1024), BF),
            vmem((TOK, 1024), F32),
            dma((NCH,)), dma((2,)), dma((2,)), dma((4,)),
            dma((2, NS)), dma((2, NS)), dma((2, XN - 1)), dma((2, XN - 1)),
            dma((2, NS)), dma((2, NS)), dma((HERE,)), dma((HERE,)),
        ],
        compiler_params=pltpu.CompilerParams(
            collective_id=0, has_side_effects=True, vmem_limit_bytes=56 * 1024 * 1024
        ),
    )(tokens, w_query, w_key, w_value, w_out)


def solution(mesh):
    in_specs = (P("seq", None), P(None, "head"), P(None, "head"), P(None, "head"), P())
    return jax.shard_map(
        per_device, mesh=mesh, in_specs=in_specs, out_specs=P("seq", "head"), check_vma=False
    )
```

time: 46.9 us -> 37.3 us (0.80)
  Pallas kernels: 43.7 us -> 35.9 us
  local copies, waits for them, and re-layouts: 3.08 us -> 1.32 us
    pallas_call x1, Pallas kernels: 43.7 us -> 35.9 us  [per_device(): pl.pallas_call(kernel, out_shape=pltpu.VMEM((TOK, 1024), BF), in_specs=[h...]
    unnamed x1, local copies, waits for them, and re-layouts: 3.08 us -> 1.32 us
where the time goes in v1:
time: 37.3 us; the launch traced here: 37.2 us
  Pallas kernels  35.9 us (96%)
  local copies, waits for them, and re-layouts  1.32 us (4%)
    pallas_call x1, Pallas kernels, per_device(): pl.pallas_call(kernel, out_shape=pltpu.VMEM((TOK, 1024), BF), in_specs=[h...  35.9 us
    unnamed x1, local copies, waits for them, and re-layouts  1.32 us

profile of v1, /device:TPU:1, one launch (start us, length us, event | category | flops | bytes accessed | tf_op | source)
XLA Modules:
  0.0 37.2 jit_solution(11332312039940949451)
XLA Ops:
  0.0 35.9 %shard_map.55 = bf16[1024,1024]{1,0:T(8,128)(2,1)S(1)} custom-call(bf16[1024,2048]{1,0:T(8,128)(2,1)} %tok_hbm.1, bf16[2048,128]{1,0:T(8,128)(2,1)} %wq_hbm.1, bf16[2048,128]{1,0:T(8,128)(2,1)} %wk_hbm.1, bf16[2048,1024]{1,0:T(8,128)(2,1)} %wv_hbm.1, bf16[2048,2048]{1,0:T(8,128)(2,1)} %wo_hbm.1), custom_call_target="tpu_custom_call" | custom-call | tf_op jit(solution)/shard_map/pallas_call | solution.py:351
  35.9 1.3 %copy.7 = bf16[1024,1024]{1,0:T(8,128)(2,1)} copy(bf16[1024,1024]{1,0:T(8,128)(2,1)S(1)} %shard_map.55) | data formatting | bytes 4194304

commit v2 on v1

--- a/solution.py
+++ b/solution.py
@@ -127,15 +127,15 @@
     def state_copy(g, i):
         to = chip(i)
         return pltpu.make_async_remote_copy(
-            src_ref=sbuf.at[g * PLANE + to], dst_ref=rbuf.at[g, me], send_sem=s_send.at[g, i],
-            recv_sem=s_recv.at[g, i], device_id={"seq": xp * PLANE + to}, device_id_type=MESH,
-        )
-
-    def state_arrival(g, i):
-        come = chip(i, -1)
-        return pltpu.make_async_remote_copy(
-            src_ref=sbuf.at[g * PLANE + come], dst_ref=rbuf.at[g, come], send_sem=s_send.at[g, i],
-            recv_sem=s_recv.at[g, i], device_id={"seq": xp * PLANE + come}, device_id_type=MESH,
+            src_ref=sbuf.at[g * PLANE + to], dst_ref=rbuf.at[g, me], send_sem=s_send.at[g],
+            recv_sem=s_recv.at[g], device_id={"seq": xp * PLANE + to}, device_id_type=MESH,
+        )
+
+    def all_states(g):
+        return pltpu.make_async_remote_copy(
+            src_ref=sbuf.at[pl.ds(g * PLANE, NS)], dst_ref=rbuf.at[g, pl.ds(0, NS)],
+            send_sem=s_send.at[g], recv_sem=s_recv.at[g],
+            device_id={"seq": xp * PLANE + chip(0)}, device_id_type=MESH,
         )
 
     def total_copy(g, dx):
@@ -156,22 +156,29 @@
     def prefix_copy(g, i):
         to = chip(i)
         return pltpu.make_async_remote_copy(
-            src_ref=obuf.at[g, to], dst_ref=pbuf.at[g * PLANE + me], send_sem=p_send.at[g, i],
-            recv_sem=p_recv.at[g, i], device_id={"seq": xp * PLANE + to}, device_id_type=MESH,
-        )
-
-    def prefix_arrival(g, i):
-        come = chip(i, -1)
-        return pltpu.make_async_remote_copy(
-            src_ref=obuf.at[g, come], dst_ref=pbuf.at[g * PLANE + come], send_sem=p_send.at[g, i],
-            recv_sem=p_recv.at[g, i], device_id={"seq": xp * PLANE + come}, device_id_type=MESH,
+            src_ref=obuf.at[g, to], dst_ref=pbuf.at[g * PLANE + me], send_sem=p_send.at[g],
+            recv_sem=p_recv.at[g], device_id={"seq": xp * PLANE + to}, device_id_type=MESH,
+        )
+
+    def all_prefixes(g):
+        return pltpu.make_async_remote_copy(
+            src_ref=obuf.at[g, pl.ds(0, NS)], dst_ref=pbuf.at[pl.ds(g * PLANE, NS)],
+            send_sem=p_send.at[g], recv_sem=p_recv.at[g],
+            device_id={"seq": xp * PLANE + chip(0)}, device_id_type=MESH,
         )
 
     def att_copy(h):
         cols = pl.ds(h * 128, 128)
         return pltpu.make_async_remote_copy(
-            src_ref=att.at[:, cols], dst_ref=sib.at[:, cols], send_sem=a_send.at[h],
-            recv_sem=a_recv.at[h], device_id={"head": 1 - core}, device_id_type=MESH,
+            src_ref=att.at[:, cols], dst_ref=sib.at[:, cols], send_sem=a_send.at[h // 4],
+            recv_sem=a_recv.at[h // 4], device_id={"head": 1 - core}, device_id_type=MESH,
+        )
+
+    def all_att(half):
+        cols = pl.ds(half * 512, 512)
+        return pltpu.make_async_remote_copy(
+            src_ref=att.at[:, cols], dst_ref=sib.at[:, cols], send_sem=a_send.at[half],
+            recv_sem=a_recv.at[half], device_id={"head": 1 - core}, device_id_type=MESH,
         )
 
     def values(g):
@@ -250,8 +257,7 @@
             numer[h, rows, :] = r
 
     def reduce_step(g):
-        for i in range(NS):
-            state_arrival(g, i).wait_recv()
+        all_states(g).wait_recv()
         tot = rbuf[g, 0].astype(F32)
         for q in range(1, PLANE):
             tot = tot + rbuf[g, q].astype(F32)
@@ -282,8 +288,7 @@
     ones128 = jnp.ones((128, 128), BF)
 
     def finish(g):
-        for i in range(NS):
-            prefix_arrival(g, i).wait_recv()
+        all_prefixes(g).wait_recv()
         for h in range(4 * g, 4 * g + 4):
             pieces = [pbuf[4 * h + k].astype(F32) for k in range(4)]
             z = pieces[3][38:40]
@@ -303,8 +308,7 @@
         j = side * 2 + half
         wo_copy(j).wait()
         if side == 1:
-            for h in range(4 * half, 4 * half + 4):
-                att_copy(h).wait_recv()
+            all_att(half).wait_recv()
         lhs = (att, sib)[side]
         for n in range(4):
             cols = slice(n * 256, (n + 1) * 256)
@@ -315,6 +319,15 @@
                 acc[:, cols] = r
             else:
                 out[:, cols] = r.astype(BF)
+
+    def drain():
+        for g in range(2):
+            all_states(g).wait_send()
+            all_prefixes(g).wait_send()
+            for dx in range(1, XN):
+                pl.when(xp + dx < XN)(total_copy(g, dx).wait_send)
+        for half in range(2):
+            all_att(half).wait_send()
 
     for g in range(2):
         values(g)
@@ -329,19 +342,11 @@
         slot(h + 1)
     finish(0)
     project(0, 0, 0)
-    project(1, 0, 1)
     finish(1)
-    project(0, 1, 2)
+    project(0, 1, 1)
+    project(1, 0, 2)
     project(1, 1, 3)
-
-    for g in range(2):
-        for i in range(NS):
-            state_copy(g, i).wait_send()
-            prefix_copy(g, i).wait_send()
-        for dx in range(1, XN):
-            pl.when(xp + dx < XN)(total_copy(g, dx).wait_send)
-    for h in range(HERE):
-        att_copy(h).wait_send()
+    drain()
 
 
 def per_device(tokens, w_query, w_key, w_value, w_out):
@@ -380,8 +385,8 @@
             vmem((TOK, 1024), BF),
             vmem((TOK, 1024), F32),
             dma((NCH,)), dma((2,)), dma((2,)), dma((4,)),
-            dma((2, NS)), dma((2, NS)), dma((2, XN - 1)), dma((2, XN - 1)),
-            dma((2, NS)), dma((2, NS)), dma((HERE,)), dma((HERE,)),
+            dma((2,)), dma((2,)), dma((2, XN - 1)), dma((2, XN - 1)),
+            dma((2,)), dma((2,)), dma((2,)), dma((2,)),
         ],
         compiler_params=pltpu.CompilerParams(
             collective_id=0, has_side_effects=True, vmem_limit_bytes=56 * 1024 * 1024

time: 37.3 us -> 35.1 us (0.941)
  the two profiles are of different devices: /device:TPU:1 before, /device:TPU:6 now
where the time goes in v2:
time: 35.1 us; the launch traced here: 35 us
  Pallas kernels  33.7 us (96%)
  local copies, waits for them, and re-layouts  1.32 us (4%)
    pallas_call x1, Pallas kernels, per_device(): pl.pallas_call(kernel, out_shape=pltpu.VMEM((TOK, 1024), BF), in_specs=[h...  33.7 us
    unnamed x1, local copies, waits for them, and re-layouts  1.32 us

profile of v2, /device:TPU:6, one launch (start us, length us, event | category | flops | bytes accessed | tf_op | source)
XLA Modules:
  0.0 35.0 jit_solution(3463632724656869741)
XLA Ops:
  0.0 33.7 %shard_map.55 = bf16[1024,1024]{1,0:T(8,128)(2,1)S(1)} custom-call(bf16[1024,2048]{1,0:T(8,128)(2,1)} %tok_hbm.1, bf16[2048,128]{1,0:T(8,128)(2,1)} %wq_hbm.1, bf16[2048,128]{1,0:T(8,128)(2,1)} %wk_hbm.1, bf16[2048,1024]{1,0:T(8,128)(2,1)} %wv_hbm.1, bf16[2048,2048]{1,0:T(8,128)(2,1)} %wo_hbm.1), custom_call_target="tpu_custom_call" | custom-call | tf_op jit(solution)/shard_map/pallas_call | solution.py:356
  33.7 1.3 %copy.7 = bf16[1024,1024]{1,0:T(8,128)(2,1)} copy(bf16[1024,1024]{1,0:T(8,128)(2,1)S(1)} %shard_map.55) | data formatting | bytes 4194304

commit v3 on v2

--- a/solution.py
+++ b/solution.py
@@ -19,7 +19,7 @@
     key=lambda s: -(min(s[0], 4 - s[0]) + min(s[1], 4 - s[1])),
 )
 NS = len(SHIFTS)
-QK_PARTS = 1
+QK_PARTS = 2
 REDUCE_AT = (1, 5)
 PREFIX_AT = (5, 8)
 MESH = pl.DeviceIdType.MESH
@@ -38,7 +38,7 @@
 
 def kernel(
     tok_hbm, wq_hbm, wk_hbm, wv_hbm, wo_hbm, out,
-    tok, wqk, wv, wo, q_s, k_s, kt, ktb, v_s, phiq, pk, ea, eb, lext, numer,
+    tok, wqk, wv, wo, q_s, k_s, kt, ktb, v_s, phiq, pk, pick, lext, t_s, numer,
     sbuf, rbuf, xs, xbuf, obuf, pbuf, pre, att, sib, acc,
     tok_sem, wqk_sem, wv_sem, wo_sem,
     s_send, s_recv, x_send, x_recv, p_send, p_recv, a_send, a_recv,
@@ -71,6 +71,7 @@
         wqk_copy(j).start()
     for b in range(NCH):
         tok_copy(b).start()
+    wv_copy(0).start()
 
     barrier = pltpu.get_barrier_semaphore()
 
@@ -95,23 +96,17 @@
 
     row = iota((256, 256), 0)
     col = iota((256, 256), 1)
-    lane_i = col & 15
-    lane_d = (col >> 4) - 1
-    ea[...] = jnp.where((row == 128 + lane_i) & (col < 152), 1.0, 0.0).astype(BF)
-    eb[...] = jnp.where(
-        (row == 128 + ((lane_i + lane_d) & 15)) & (col >= 16) & (col < 152), 1.0, 0.0
-    ).astype(BF)
+    shift = jnp.where(col < 128, 0, (col - 128) >> 4)
+    pick[...] = jnp.where(row == 128 + (((col & 15) + shift) & 15), 1.0, 0.0).astype(BF)
 
     for j in range(2):
         wqk_copy(j).wait()
+    for b in range(NCH):
+        tok_copy(b).wait()
+    wv_copy(1).start()
     for part in range(QK_PARTS):
-        each = NCH // QK_PARTS
-        for b in range(part * each, part * each + each):
-            tok_copy(b).wait()
-        if part == 0:
-            for j in range(2):
-                wv_copy(j).start()
-        rows = slice(part * each * CHUNK, (part + 1) * each * CHUNK)
+        each = TOK // QK_PARTS
+        rows = slice(part * each, (part + 1) * each)
         qk = dot(tok[rows, :], wqk[...])
         q_s[rows, :] = qk[:, :128].astype(BF)
         k_s[rows, :] = qk[:, 128:].astype(BF)
@@ -195,10 +190,10 @@
         for j in range(4):
             h = 4 * g + j
             u = kt[h * 16 : (h + 1) * 16, :]
-            pk[j, 0:16, :] = (u * 0.5).astype(BF)
+            pk[j, 128:144, :] = (u * 0.5).astype(BF)
             for d in range(8):
                 other = u if d == 0 else pltpu.roll(u, 16 - d, 0)
-                pk[j, 16 + 16 * d : 32 + 16 * d, :] = (u * other * C2).astype(BF)
+                pk[j, 16 * d : 16 * d + 16, :] = (u * other * C2).astype(BF)
             last = u * pltpu.roll(u, 8, 0) * C2
             last = jnp.where(row16w < 8, last, jnp.where(row16w == 8, 1.0, 0.0))
             pk[j, 144:160, :] = last.astype(BF)
@@ -228,33 +223,39 @@
             state_copy(g, i).start()
         rbuf[g, me] = sbuf[g * PLANE + me]
 
-    lane = iota((1, 256), 1)
-    c1 = jnp.where(lane < 16, 1.0, 0.0)
-    c0 = jnp.where(lane == 152, 2.0, 0.0)
-    scale = jnp.where(lane < 16, 1.0, jnp.where(lane < 32, 2.0 * C2, 4.0 * C2))
     lane128 = iota((1, 128), 1)
+    scale = jnp.where(lane128 < 16, 2.0 * C2, 4.0 * C2)
+    const = jnp.where(lane128 == 24, 2.0, 0.0)
     causal = iota((CHUNK, CHUNK), 1) <= iota((CHUNK, CHUNK), 0)
 
+    def weights(h, b):
+        rows = slice(b * CHUNK, (b + 1) * CHUNK)
+        low = 128 - 16 * h
+        qb = q_s[rows, :]
+        both = dot(qb, pick[low : low + 128, :])
+        own = jnp.where((lane128 >> 4) == h, 0.25, 0.0).astype(BF)
+        t = dot(qb * own, ktb[:, rows]) + 1.0
+        one = both[:, :128]
+        far = one * pltpu.roll(one, 8, 1) * (4.0 * C2)
+        last = jnp.where(lane128 < 16, one, jnp.where(lane128 < 24, far, const))
+        feat = jnp.concatenate([one * both[:, 128:] * scale, last], axis=1).astype(BF)
+        phiq[h, rows, :] = feat
+        t_s[h % 2, b] = jnp.where(causal, t * t + 1.0, 0.0).astype(BF)
+
+    def collect(h, b):
+        rows = slice(b * CHUNK, (b + 1) * CHUNK)
+        vcols = slice((h % 4) * 128, (h % 4) * 128 + 128)
+        vals = jnp.concatenate([v_s[h // 4, rows, vcols], ones], axis=1)
+        r = dot(t_s[h % 2, b], vals)
+        if b > 0:
+            r = r + dot(phiq[h, rows, :FEAT], lext[h, b - 1])
+        numer[h, rows, :] = r
+
     def inside(h):
-        low = 128 - 16 * h
-        ea_h = ea[low : low + 128, :]
-        eb_h = eb[low : low + 128, :]
-        own = jnp.where((lane128 >> 4) == h, 0.25, 0.0).astype(BF)
-        vcols = slice((h % 4) * 128, (h % 4) * 128 + 128)
         for b in range(NCH):
-            rows = slice(b * CHUNK, (b + 1) * CHUNK)
-            qb = q_s[rows, :]
-            first = dot(qb, ea_h)
-            second = dot(qb, eb_h)
-            feat = (first * (second + c1) * scale + c0).astype(BF)
-            phiq[h, rows, :] = feat
-            t = dot(qb * own, ktb[:, rows]) + 1.0
-            t = jnp.where(causal, t * t + 1.0, 0.0).astype(BF)
-            vals = jnp.concatenate([v_s[h // 4, rows, vcols], ones], axis=1)
-            r = dot(t, vals)
-            if b > 0:
-                r = r + dot(feat[:, :FEAT], lext[h, b - 1])
-            numer[h, rows, :] = r
+            if h + 1 < HERE:
+                weights(h + 1, b)
+            collect(h, b)
 
     def reduce_step(g):
         all_states(g).wait_recv()
@@ -337,6 +338,8 @@
             pl.semaphore_wait(barrier, NS + XN - 1 + 1)
         send_states(g)
     slot(0)
+    for b in range(NCH):
+        weights(0, b)
     for h in range(HERE):
         inside(h)
         slot(h + 1)
@@ -371,8 +374,8 @@
             vmem((HERE, TOK, 256), BF),
             vmem((4, FEAT, TOK), BF),
             vmem((256, 256), BF),
-            vmem((256, 256), BF),
             vmem((HERE, NCH - 1, FEAT, 256), BF),
+            vmem((2, NCH, CHUNK, CHUNK), BF),
             vmem((HERE, TOK, 256), F32),
             vmem((2 * PLANE, PIECE, 128), BF),
             vmem((2, PLANE, PIECE, 128), BF),

time: 35.1 us -> 32.8 us (0.934)
  Pallas kernels: 33.7 us -> 31.4 us
    pallas_call x1, Pallas kernels: 33.7 us -> 31.4 us  [per_device(): pl.pallas_call(kernel, out_shape=pltpu.VMEM((TOK, 1024), BF), in_specs=[h...]
where the time goes in v3:
time: 32.8 us; the launch traced here: 32.7 us
  Pallas kernels  31.4 us (96%)
  local copies, waits for them, and re-layouts  1.32 us (4%)
    pallas_call x1, Pallas kernels, per_device(): pl.pallas_call(kernel, out_shape=pltpu.VMEM((TOK, 1024), BF), in_specs=[h...  31.4 us
    unnamed x1, local copies, waits for them, and re-layouts  1.32 us

profile of v3, /device:TPU:6, one launch (start us, length us, event | category | flops | bytes accessed | tf_op | source)
XLA Modules:
  0.0 32.7 jit_solution(9884310671278948719)
XLA Ops:
  0.0 31.4 %shard_map.55 = bf16[1024,1024]{1,0:T(8,128)(2,1)S(1)} custom-call(bf16[1024,2048]{1,0:T(8,128)(2,1)} %tok_hbm.1, bf16[2048,128]{1,0:T(8,128)(2,1)} %wq_hbm.1, bf16[2048,128]{1,0:T(8,128)(2,1)} %wk_hbm.1, bf16[2048,1024]{1,0:T(8,128)(2,1)} %wv_hbm.1, bf16[2048,2048]{1,0:T(8,128)(2,1)} %wo_hbm.1), custom_call_target="tpu_custom_call" | custom-call | tf_op jit(solution)/shard_map/pallas_call | solution.py:359
  31.4 1.3 %copy.7 = bf16[1024,1024]{1,0:T(8,128)(2,1)} copy(bf16[1024,1024]{1,0:T(8,128)(2,1)S(1)} %shard_map.55) | data formatting | bytes 4194304

commit v4 on v3

--- a/solution.py
+++ b/solution.py
@@ -21,7 +21,7 @@
 NS = len(SHIFTS)
 QK_PARTS = 2
 REDUCE_AT = (1, 5)
-PREFIX_AT = (5, 8)
+PREFIX_AT = (5, 7)
 MESH = pl.DeviceIdType.MESH
 C2 = 1.0 / (32.0**0.5)
 BF = jnp.bfloat16

time: 32.8 us -> 32.8 us (level)
  no operation moved by 1% of the time
where the time goes in v4:
time: 32.8 us; the launch traced here: 32.7 us
  Pallas kernels  31.4 us (96%)
  local copies, waits for them, and re-layouts  1.32 us (4%)
    pallas_call x1, Pallas kernels, per_device(): pl.pallas_call(kernel, out_shape=pltpu.VMEM((TOK, 1024), BF), in_specs=[h...  31.4 us
    unnamed x1, local copies, waits for them, and re-layouts  1.32 us

profile of v4, /device:TPU:6, one launch (start us, length us, event | category | flops | bytes accessed | tf_op | source)
XLA Modules:
  0.0 32.7 jit_solution(8534017686259665483)
XLA Ops:
  0.0 31.4 %shard_map.55 = bf16[1024,1024]{1,0:T(8,128)(2,1)S(1)} custom-call(bf16[1024,2048]{1,0:T(8,128)(2,1)} %tok_hbm.1, bf16[2048,128]{1,0:T(8,128)(2,1)} %wq_hbm.1, bf16[2048,128]{1,0:T(8,128)(2,1)} %wk_hbm.1, bf16[2048,1024]{1,0:T(8,128)(2,1)} %wv_hbm.1, bf16[2048,2048]{1,0:T(8,128)(2,1)} %wo_hbm.1), custom_call_target="tpu_custom_call" | custom-call | tf_op jit(solution)/shard_map/pallas_call | solution.py:359
  31.4 1.3 %copy.7 = bf16[1024,1024]{1,0:T(8,128)(2,1)} copy(bf16[1024,1024]{1,0:T(8,128)(2,1)S(1)} %shard_map.55) | data formatting | bytes 4194304
